TPU v7x, 32 devices: a whole 2x2x4 slice. The times are simulated.
32 devices in a mesh: dom: 8 (over z, y), sub: 4 (over x, core).
Axes of the slice: x: 2, y: 2, z: 4, core: 2. Of those that a mesh axis runs over, the one named last changes fastest.
Arguments:
- positions: float32 [3, 131072], P(None, ('dom', 'sub')), may hold values from -20 to 20
- mass: float32 [131072], P(('dom', 'sub')), may hold values from 3 to 6
- local_tiles: float32 [2048, 128, 128], P(('dom', 'sub')), as said below
- local_rows: int32 [2048], P(('dom', 'sub')), may hold values from 0 to 31, as said below
- local_cols: int32 [2048], P(('dom', 'sub')), may hold values from 0 to 31, as said below
- live_tiles: int32 [32], P(('dom', 'sub')), may hold values from 32 to 64, as said below
- dom_tiles: float32 [1024, 128, 128], P(('dom', 'sub')), as said below
- dom_cols: int32 [1024], P(('dom', 'sub')), may hold values from 0 to 31
- dom_slots: int32 [1024], P(('dom', 'sub')), may hold values from 0 to 255, as said below
- dom_rows: int32 [8192], P(('dom', 'sub')), may hold values from 0 to 31, as said below
- sub_tiles: float32 [1536, 128, 128], P(('dom', 'sub')), as said below
- sub_cols: int32 [1536], P(('dom', 'sub')), may hold values from 0 to 31
- sub_slots: int32 [1536], P(('dom', 'sub')), may hold values from 0 to 63, as said below
- sub_rows: int32 [2048], P(('dom', 'sub')), may hold values from 0 to 31, as said below
- precond: float32 [1024, 128, 128], P(('dom', 'sub')), may hold values from -0.05 to 0.3, as said below
Outputs:
- solution: float32 [3, 131072], P(None, ('dom', 'sub'))
- residual: float32 [3, 131072], P(None, ('dom', 'sub'))
Inputs may be any that keep to these rules, and one draw needn't show every extreme that they name: Device d uses the first live_tiles[d] of its 64 interior tiles, an even number; some device uses all of them. `local_tiles`: interior tiles come in pairs 2i, 2i + 1 of a device: the second is the transpose of the first. `local_rows`: tile 2i + 1 of a device has the block row and column of tile 2i swapped. `local_cols`: tile 2i + 1 of a device has the block row and column of tile 2i swapped. `dom_slots`: the destination group of a tile differs from its device's dom index in exactly one of its 3 bits; no two tiles of a device share a slot. `dom_rows`: entries for slots that no tile fills are arbitrary blocks of the receiver. `dom_tiles`: every coupling tile that reaches block row r of a device from block column c of another has a transposed tile on the receiver, from its block column r, that reaches block row c of the sender; so A is symmetric. `sub_slots`: the destination partition of a tile lies in its device's group and is not its device's own; no two tiles of a device share a slot. `sub_rows`: entries for slots that no tile fills are arbitrary blocks of the receiver. `sub_tiles`: every such tile has a transposed partner on the receiving partition that is routed back to the sender's block column. `precond`: every block is symmetric and positive definite.
All inputs are finite; a program needn't handle non-finite values.
Results may differ from a plain program's by a relative error of at most 0.0003.
Values sent between devices are 32-bit elements; how exact they have to be, the bound alone decides.
A program may use at most 64 MiB of HBM per device.

v0:
```python
import functools

import jax
import jax.numpy as jnp
from jax import lax
from jax.experimental import pallas as pl
from jax.experimental.pallas import tpu as pltpu
from jax.sharding import PartitionSpec as P

ITERS = 3
SHIFT = 1.0
CHUNK = 16
F32 = jnp.float32
BF16 = jnp.bfloat16
MESH = pl.DeviceIdType.MESH


def high(value):
    return value.astype(BF16).astype(F32)


def kernel(count_dom, count_sub, bits, pos_hbm, mass_hbm, local_rows, live, dom_rows, dom_slots, sub_rows, sub_slots,
           local_cols_hbm, dom_cols_hbm, sub_cols_hbm, local_hbm, dom_hbm, sub_hbm, pre_hbm, sol_hbm, res_hbm,
           stage, weights, place, vec, image, expanded, products, index, send_dom, recv_dom, send_sub, recv_sub,
           sums_sub, sums_dom, own, load_sem, dom_send_sem, dom_recv_sem, sub_send_sem, sub_recv_sem,
           red_send, red_recv, pos_ref, mass_ref, local_cols, dom_cols, sub_cols, sol_ref, res_ref,
           small_sem, far_sem):
    lt, ld, ls, nb = local_hbm.shape[0], dom_hbm.shape[0], sub_hbm.shape[0], pre_hbm.shape[0]
    tile = pre_hbm.shape[1]
    width_dom = dom_rows.shape[0] // count_dom
    width_sub = sub_rows.shape[0] // count_sub
    a = lax.axis_index("dom")
    b = lax.axis_index("sub")
    tiles = lt + ld + ls

    def partner_dom(j):
        bit = 1 << j
        return a + bit - 2 * bit * ((a // bit) % 2)

    small = []
    for source, target in ((pos_hbm, pos_ref), (local_cols_hbm, local_cols), (dom_cols_hbm, dom_cols),
                           (sub_cols_hbm, sub_cols), (mass_hbm, mass_ref)):
        copy = pltpu.make_async_copy(source, target, small_sem.at[len(small)])
        copy.start()
        small.append(copy)

    barrier = pltpu.get_barrier_semaphore()
    for j in range(bits):
        pl.semaphore_signal(barrier, inc=1, device_id=(partner_dom(j), b), device_id_type=MESH)
    for o in range(1, count_sub):
        pl.semaphore_signal(barrier, inc=1, device_id=(a, (b + o) % count_sub), device_id_type=MESH)

    loads = {}
    for start, source in ((0, local_hbm), (tiles, pre_hbm), (lt + ld, sub_hbm), (lt, dom_hbm)):
        for first in range(0, source.shape[0], CHUNK):
            copy = pltpu.make_async_copy(source.at[pl.ds(first, CHUNK)], stage.at[pl.ds(start + first, CHUNK)],
                                         load_sem.at[(start + first) // CHUNK])
            copy.start()
            loads[(start + first) // CHUNK] = copy

    sub8 = lax.broadcasted_iota(jnp.int32, (8, tile), 0)
    upper = sub8 < 4
    zero1 = jnp.zeros((1, tile), F32)

    def doubled(three):
        return jnp.concatenate([three, zero1, three, zero1], axis=0)

    def split_rows(value):
        h = high(value)
        return jnp.where(upper, h, value - h)

    for copy in small:
        copy.wait()

    for k in range(nb):
        vec[0, k] = doubled(pos_ref[:, k * tile:(k + 1) * tile])

    def exchange(k):
        copies = []
        for j in reversed(range(bits)):
            other = partner_dom(j)
            for s in range(width_dom):
                send_dom[k, j, 3 * s:3 * s + 3, :] = vec[k, dom_rows[other * width_dom + s], 0:3, :]
            copy = pltpu.make_async_remote_copy(
                src_ref=send_dom.at[k, j], dst_ref=recv_dom.at[k, j], send_sem=dom_send_sem.at[k, j],
                recv_sem=dom_recv_sem.at[k, j], device_id=(other, b), device_id_type=MESH)
            copy.start()
            copies.append(copy)
        for o in range(1, count_sub):
            other = (b + o) % count_sub
            for s in range(width_sub):
                send_sub[k, o - 1, 3 * s:3 * s + 3, :] = vec[k, sub_rows[other * width_sub + s], 0:3, :]
            copy = pltpu.make_async_remote_copy(
                src_ref=send_sub.at[k, o - 1], dst_ref=recv_sub.at[k, o - 1], send_sem=sub_send_sem.at[k, o - 1],
                recv_sem=sub_recv_sem.at[k, o - 1], device_id=(a, other), device_id_type=MESH)
            copy.start()
            copies.append(copy)
        return copies

    def expand_own(k):
        for n in range(nb):
            expanded[n] = split_rows(vec[k, n])

    def expand_received(k, copies):
        for o in range(1, count_sub):
            copies[bits + o - 1].wait_recv()
            base = nb + count_dom * width_dom + ((b + count_sub - o) % count_sub) * width_sub
            for s in range(width_sub):
                expanded[base + s] = split_rows(doubled(recv_sub[k, o - 1, 3 * s:3 * s + 3, :]))

    def expand_received_dom(k, copies):
        for j in rounds[k]:
            pl.semaphore_wait(far_sem.at[j], 1)
        for j in range(bits):
            copies[bits - 1 - j].wait_recv()
            base = nb + partner_dom(j) * width_dom
            for s in range(width_dom):
                expanded[base + s] = split_rows(doubled(recv_dom[k, j, 3 * s:3 * s + 3, :]))

    def multiply(left, right, pair):
        rows = jnp.concatenate([left, right], axis=0).astype(BF16)
        out = jnp.dot(jnp.concatenate([rows, rows], axis=1), weights[pair], preferred_element_type=F32)
        return out[0:8, 0:tile], out[8:16, tile:2 * tile]

    def one_pair(p):
        left, right = multiply(expanded[index[2 * p]], expanded[index[2 * p + 1]], p)
        both = jnp.concatenate([left, right], axis=0)
        h = both.astype(BF16)
        low = (both - h.astype(F32)).astype(BF16)
        products[pl.ds(pl.multiple_of(16 * p, 16), 16), :] = jnp.concatenate([h, low], axis=1)

    def run_pairs(first, last):
        unroll = last - first if last - first <= 24 else 16
        def body(i, carry):
            for u in range(unroll):
                one_pair(first + i * unroll + u)
            return carry
        lax.fori_loop(0, (last - first) // unroll, body, 0)

    def scatter(first, last):
        out = jnp.dot(place[:, 8 * first:8 * last], products[8 * first:8 * last, :], preferred_element_type=F32)
        return (out[:, 0:tile] + out[:, tile:2 * tile]).reshape(nb, 8, tile)

    def apply_pre(k):
        for p in range(nb // 2):
            left, right = multiply(split_rows(image[k, 2 * p]), split_rows(image[k, 2 * p + 1]), tiles // 2 + p)
            left = left + pltpu.roll(left, 4, 0)
            right = right + pltpu.roll(right, 4, 0)
            if k > 0:
                left = left - SHIFT * vec[k, 2 * p]
                right = right - SHIFT * vec[k, 2 * p + 1]
            vec[k + 1, 2 * p] = left
            vec[k + 1, 2 * p + 1] = right

    expand_own(0)

    def fill(t, carry):
        index[t] = local_rows[t]
        return carry
    lax.fori_loop(0, lt, fill, 0)

    def fill_dom(t, carry):
        index[lt + t] = nb + dom_slots[t]
        return carry
    lax.fori_loop(0, ld, fill_dom, 0)

    def fill_sub(t, carry):
        index[lt + ld + t] = nb + count_dom * width_dom + sub_slots[t]
        return carry
    lax.fori_loop(0, ls, fill_sub, 0)

    column = 0
    for cols in (local_cols, dom_cols, sub_cols):
        n = cols.shape[1]
        reach = (lax.broadcasted_iota(jnp.int32, (n, 8 * n), 1) // 8
                 == lax.broadcasted_iota(jnp.int32, (n, 8 * n), 0)).astype(F32).astype(BF16)
        spread = jnp.dot(jnp.broadcast_to(cols[...].astype(F32), (8, n)).astype(BF16), reach,
                         preferred_element_type=F32)
        pattern = ((lax.broadcasted_iota(jnp.int32, (8, 8 * n), 1) % 4)
                   == (lax.broadcasted_iota(jnp.int32, (8, 8 * n), 0) % 4))
        spread = jnp.where(pattern, spread, -1.0)
        for k in range(0, nb, 2):
            low = jnp.where(jnp.abs(spread - k) < 0.5, 1.0, 0.0)
            up = jnp.where(jnp.abs(spread - (k + 1)) < 0.5, 1.0, 0.0)
            place[8 * k:8 * k + 16, column:column + 8 * n] = jnp.concatenate([low, up], axis=0).astype(BF16)
        column += 8 * n

    used = live[0]

    def convert(p, masked):
        for side in range(2):
            value = stage[2 * p + side]
            if masked:
                value = value * (2 * p + side < used).astype(F32)
            h = value.astype(BF16)
            weights[p, 0:tile, side * tile:(side + 1) * tile] = h
            weights[p, tile:2 * tile, side * tile:(side + 1) * tile] = (value - h.astype(F32)).astype(BF16)

    def arrive(first, last, masked=False, multiplied=False, unroll=4):
        for c in range(first // CHUNK, last // CHUNK):
            loads[c].wait()

            def body(i, carry):
                for u in range(unroll):
                    convert(c * CHUNK // 2 + i * unroll + u, masked)
                if multiplied:
                    for u in range(unroll):
                        one_pair(c * CHUNK // 2 + i * unroll + u)
                return carry
            lax.fori_loop(0, CHUNK // 2 // unroll, body, 0)

    pairs = [(i, j) for i in range(ITERS) for j in range(i, ITERS)]

    def inner(sums):
        totals = [jnp.zeros((8, tile), F32)] * len(sums)
        for n in range(nb):
            vectors = {i: vec[i + 1, n] for i in {x for x, _ in sums}}
            images = {j: image[j, n] for j in {y for _, y in sums}}
            totals = [t + vectors[x] * images[y] for t, (x, y) in zip(totals, sums)]
        return [jnp.sum(t, axis=1, keepdims=True) for t in totals]

    early = [(i, j + 1) for i, j in pairs if j + 1 < ITERS] + [(i, 0) for i in range(ITERS)]
    late = [(i, j + 1) for i, j in pairs if j + 1 == ITERS]

    copies = []
    rounds = [range(0, 0)] + [range((k - 1) * bits // ITERS, k * bits // ITERS) for k in range(1, ITERS + 1)]
    for k in range(ITERS + 1):
        if k > 0:
            copies.append(exchange(k))
            for j in rounds[k]:
                pl.semaphore_signal(far_sem.at[j], inc=1, device_id=(partner_dom(j), b), device_id_type=MESH)
            expand_own(k)
            run_pairs(0, lt // 2)
        else:
            pl.semaphore_wait(barrier, bits + count_sub - 1)
            copies.append(exchange(0))
            arrive(0, lt // 2, True, True)
            arrive(lt // 2, lt, True, True)
        part = scatter(0, lt)
        for n in range(nb):
            if k > 0:
                image[k, n] = part[n] + mass_ref[n:n + 1, :] * vec[k, n]
            else:
                image[k, n] = part[n]
        if k == ITERS:
            early_sums = inner(early)
        if k == 0:
            arrive(tiles, tiles + nb)
            arrive(lt + ld, tiles)
            arrive(lt, lt + ld)
        expand_received(k, copies[k])
        run_pairs((lt + ld) // 2, tiles // 2)
        part = scatter(lt + ld, tiles)
        for n in range(nb):
            image[k, n] = image[k, n] + part[n]
        expand_received_dom(k, copies[k])
        run_pairs(lt // 2, (lt + ld) // 2)
        part = scatter(lt, lt + ld)
        for n in range(nb):
            if k > 0:
                image[k, n] = image[k, n] + part[n]
            else:
                image[k, n] = -(image[k, n] + part[n])
        if k < ITERS:
            apply_pre(k)

    totals = early_sums + inner(late)
    order = early + late
    lane = lax.broadcasted_iota(jnp.int32, (8, tile), 1)
    packed = jnp.zeros((8, tile), F32)
    for i, value in enumerate(totals):
        packed = jnp.where(lane == i, value, packed)

    own[0] = packed
    stage_copies = []
    for o in range(1, count_sub):
        copy = pltpu.make_async_remote_copy(
            src_ref=own.at[0], dst_ref=sums_sub.at[o - 1], send_sem=red_send.at[o - 1],
            recv_sem=red_recv.at[o - 1], device_id=(a, (b + o) % count_sub), device_id_type=MESH)
        copy.start()
        stage_copies.append(copy)
    for o in range(1, count_sub):
        stage_copies[o - 1].wait_recv()
    for o in range(1, count_sub):
        packed = packed + sums_sub[o - 1]
    own[1] = packed
    for o in range(1, count_dom):
        q = count_sub - 1 + o - 1
        copy = pltpu.make_async_remote_copy(
            src_ref=own.at[1], dst_ref=sums_dom.at[o - 1], send_sem=red_send.at[q],
            recv_sem=red_recv.at[q], device_id=((a + o) % count_dom, b), device_id_type=MESH)
        copy.start()
        stage_copies.append(copy)
    for o in range(1, count_dom):
        stage_copies[count_sub - 1 + o - 1].wait_recv()
    for o in range(1, count_dom):
        packed = packed + sums_dom[o - 1]

    def pick(i):
        return jnp.sum(jnp.where(lane == i, packed, 0.0), axis=1, keepdims=True) + jnp.zeros((8, tile), F32)

    gram = {}
    for x, y in pairs:
        gram[x, y] = gram[y, x] = pick(order.index((x, y + 1)))
    first = [pick(order.index((i, 0))) for i in range(ITERS)]

    def add(x, y):
        return y if x is None else x if y is None else x + y

    direction = [jnp.ones((8, tile), F32)] + [None] * (ITERS - 1)
    coefs = [None] * ITERS
    current = first[0]
    for it in range(ITERS):
        used_terms = [i for i in range(ITERS) if direction[i] is not None]
        curvature = None
        for i in used_terms:
            inner = None
            for j in used_terms:
                inner = add(inner, gram[i, j] * direction[j])
            curvature = add(curvature, direction[i] * inner)
        step = current / curvature
        for i in used_terms:
            coefs[i] = add(coefs[i], step * direction[i])
        if it + 1 < ITERS:
            smooth = [jnp.ones((8, tile), F32)] + [None] * (ITERS - 1)
            for j in range(it + 1):
                smooth[j + 1] = add(smooth[j + 1], -coefs[j])
                smooth[j] = add(smooth[j], -SHIFT * coefs[j])
            following = None
            for i in range(ITERS):
                if smooth[i] is None:
                    continue
                inner = first[i]
                for j in range(it + 1):
                    inner = inner - coefs[j] * gram[i, j]
                following = add(following, smooth[i] * inner)
            ratio = following / current
            direction = [add(s, None if d is None else ratio * d) for s, d in zip(smooth, direction)]
            current = following

    for n in range(nb):
        x = vec[0, n]
        r = image[0, n]
        for i in range(ITERS):
            x = x + coefs[i] * vec[i + 1, n]
            r = r - coefs[i] * image[i + 1, n]
        sol_ref[:, n * tile:(n + 1) * tile] = x[0:3, :]
        res_ref[:, n * tile:(n + 1) * tile] = r[0:3, :]

    final = [pltpu.make_async_copy(sol_ref, sol_hbm, small_sem.at[0]),
             pltpu.make_async_copy(res_ref, res_hbm, small_sem.at[1])]
    for copy in final:
        copy.start()
    for copy in final:
        copy.wait()

    for group in copies:
        for copy in group:
            copy.wait_send()
    for copy in stage_copies:
        copy.wait_send()


def finish(sol_in, res_in, sol_ref, res_ref):
    sol_ref[...] = sol_in[...]
    res_ref[...] = res_in[...]


def on_device(positions, mass, local_tiles, local_rows, local_cols, live_tiles, dom_tiles, dom_cols, dom_slots,
              dom_rows, sub_tiles, sub_cols, sub_slots, sub_rows, precond):
    count_dom = lax.axis_size("dom")
    count_sub = lax.axis_size("sub")
    bits = count_dom.bit_length() - 1
    nb, tile = precond.shape[0], precond.shape[1]
    lt, ld, ls = local_tiles.shape[0], dom_tiles.shape[0], sub_tiles.shape[0]
    tiles = lt + ld + ls
    width_dom = dom_rows.shape[0] // count_dom
    width_sub = sub_rows.shape[0] // count_sub
    vmem = pl.BlockSpec(memory_space=pltpu.VMEM)
    smem = pl.BlockSpec(memory_space=pltpu.SMEM)
    anym = pl.BlockSpec(memory_space=pl.ANY)
    k = ITERS + 1
    n_red = count_sub + count_dom - 2
    outs = pl.pallas_call(
        functools.partial(kernel, count_dom, count_sub, bits),
        out_shape=[jax.ShapeDtypeStruct(positions.shape, F32)] * 2,
        in_specs=[anym, anym] + [smem] * 6 + [anym] * 7,
        out_specs=[anym, anym],
        scratch_shapes=[
            pltpu.VMEM((tiles + nb, tile, tile), F32),
            pltpu.VMEM(((tiles + nb) // 2, 2 * tile, 2 * tile), BF16),
            pltpu.VMEM((8 * nb, 8 * tiles), BF16),
            pltpu.VMEM((k, nb, 8, tile), F32),
            pltpu.VMEM((k, nb, 8, tile), F32),
            pltpu.VMEM((nb + count_dom * width_dom + count_sub * width_sub, 8, tile), F32),
            pltpu.VMEM((8 * tiles, 2 * tile), BF16),
            pltpu.SMEM((tiles,), jnp.int32),
            pltpu.VMEM((k, bits, 3 * width_dom, tile), F32),
            pltpu.VMEM((k, bits, 3 * width_dom, tile), F32),
            pltpu.VMEM((k, count_sub - 1, 3 * width_sub, tile), F32),
            pltpu.VMEM((k, count_sub - 1, 3 * width_sub, tile), F32),
            pltpu.VMEM((count_sub - 1, 8, tile), F32),
            pltpu.VMEM((count_dom - 1, 8, tile), F32),
            pltpu.VMEM((2, 8, tile), F32),
            pltpu.SemaphoreType.DMA(((tiles + nb) // CHUNK,)),
            pltpu.SemaphoreType.DMA((k, bits)),
            pltpu.SemaphoreType.DMA((k, bits)),
            pltpu.SemaphoreType.DMA((k, count_sub - 1)),
            pltpu.SemaphoreType.DMA((k, count_sub - 1)),
            pltpu.SemaphoreType.DMA((n_red,)),
            pltpu.SemaphoreType.DMA((n_red,)),
            pltpu.VMEM(positions.shape, F32),
            pltpu.VMEM((nb, tile), F32),
            pltpu.VMEM((1, lt), jnp.int32),
            pltpu.VMEM((1, ld), jnp.int32),
            pltpu.VMEM((1, ls), jnp.int32),
            pltpu.VMEM(positions.shape, F32),
            pltpu.VMEM(positions.shape, F32),
            pltpu.SemaphoreType.DMA((5,)),
            pltpu.SemaphoreType.REGULAR((bits,)),
        ],
        compiler_params=pltpu.CompilerParams(
            collective_id=0, has_side_effects=True, vmem_limit_bytes=60 * 1024 * 1024),
        name="fairing",
    )(positions, mass.reshape(nb, tile), local_rows, live_tiles, dom_rows, dom_slots, sub_rows, sub_slots,
      local_cols.reshape(1, lt), dom_cols.reshape(1, ld), sub_cols.reshape(1, ls),
      local_tiles, dom_tiles, sub_tiles, precond)
    return pl.pallas_call(
        finish,
        out_shape=[jax.ShapeDtypeStruct(positions.shape, F32)] * 2,
        in_specs=[vmem, vmem],
        out_specs=[vmem, vmem],
        name="finish",
    )(*outs)


def solution(mesh):
    split = P(("dom", "sub"))
    tiled = P(("dom", "sub"), None, None)
    placed = (P(None, ("dom", "sub")), split, tiled, split, split, split, tiled, split, split, split, tiled, split,
              split, split, tiled)
    return jax.shard_map(
        on_device,
        mesh=mesh,
        in_specs=placed,
        out_specs=(P(None, ("dom", "sub")), P(None, ("dom", "sub"))),
        check_vma=False,
    )
```

profile of v0, /device:TPU:0, one launch (start us, length us, event | category | flops | bytes accessed | tf_op | source)
XLA Modules:
  0.0 38.6 jit_solution(6755651691674162335)
XLA Ops:
  1.3 35.7 %fairing.1 = (f32[3,4096]{1,0:T(4,128)}, f32[3,4096]{1,0:T(4,128)}) custom-call(f32[3,4096]{1,0:T(4,128)} %pos_hbm.1, f32[32,128]{1,0:T(8,128)} %bitcast.4, s32[64]{0:T(128)} %local_rows.1, s32[1]{0:T(128)S(6)} %copy.17.live, s32[256]{0:T(256)} %dom_rows.1, s32[32]{0:T(128)} %dom_slots.1, s32[64]{0:T(128)} %sub_rows.1, s32[48]{0:T(128)} %sub_slots.1, ...), custom_call_target="tpu_custom_call" | custom-call | tf_op jit(solution)/shard_map/fairing/pallas_call | solution.py:384
  37.0 1.5 %finish.1 = (f32[3,4096]{1,0:T(4,128)}, f32[3,4096]{1,0:T(4,128)}) custom-call(f32[3,4096]{1,0:T(4,128)} %get-tuple-element.4.sol_in, f32[3,4096]{1,0:T(4,128)} %get-tuple-element.5.res_in), custom_call_target="tpu_custom_call" | custom-call | tf_op jit(solution)/shard_map/finish/pallas_call | solution.py:428
where the time goes:
time: 38.8 us; the launch traced here: 38.6 us
  Pallas kernels  37.3 us (96%)
  between operations  1.29 us (3%)
    pallas_call x1, Pallas kernels, on_device(): pl.pallas_call(functools.partial(kernel, count_dom, count_sub, bits), out...  35.7 us
    pallas_call x1, Pallas kernels, on_device(): pl.pallas_call(finish, out_shape=[jax.ShapeDtypeStruct(positions.shape, F...  1.53 us

commit v1 on v0

--- a/solution.py
+++ b/solution.py
@@ -19,16 +19,17 @@
     return value.astype(BF16).astype(F32)
 
 
-def kernel(count_dom, count_sub, bits, pos_hbm, mass_hbm, local_rows, live, dom_rows, dom_slots, sub_rows, sub_slots,
-           local_cols_hbm, dom_cols_hbm, sub_cols_hbm, local_hbm, dom_hbm, sub_hbm, pre_hbm, sol_hbm, res_hbm,
-           stage, weights, place, vec, image, expanded, products, index, send_dom, recv_dom, send_sub, recv_sub,
-           sums_sub, sums_dom, own, load_sem, dom_send_sem, dom_recv_sem, sub_send_sem, sub_recv_sem,
+def kernel(count_dom, count_sub, bits, pos_hbm, mass_hbm, local_rows_hbm, live_hbm, dom_rows_hbm, dom_slots_hbm,
+           sub_rows_hbm, sub_slots_hbm, dom_cols_flat, local_cols_hbm, dom_cols_hbm, sub_cols_hbm, local_hbm, dom_hbm, sub_hbm, pre_hbm, sol_hbm, res_hbm,
+           stage, weights, place, vec, image, expanded, products, local_rows, live, dom_rows, dom_slots, sub_rows,
+           sub_slots, dom_cols_s, send_dom, recv_dom, send_sub, recv_sub,
+           sums, own, load_sem, dom_send_sem, dom_recv_sem, sub_send_sem, sub_recv_sem,
            red_send, red_recv, pos_ref, mass_ref, local_cols, dom_cols, sub_cols, sol_ref, res_ref,
            small_sem, far_sem):
     lt, ld, ls, nb = local_hbm.shape[0], dom_hbm.shape[0], sub_hbm.shape[0], pre_hbm.shape[0]
     tile = pre_hbm.shape[1]
-    width_dom = dom_rows.shape[0] // count_dom
-    width_sub = sub_rows.shape[0] // count_sub
+    width_dom = dom_rows_hbm.shape[0] // count_dom
+    width_sub = sub_rows_hbm.shape[0] // count_sub
     a = lax.axis_index("dom")
     b = lax.axis_index("sub")
     tiles = lt + ld + ls
@@ -38,8 +39,10 @@
         return a + bit - 2 * bit * ((a // bit) % 2)
 
     small = []
-    for source, target in ((pos_hbm, pos_ref), (local_cols_hbm, local_cols), (dom_cols_hbm, dom_cols),
-                           (sub_cols_hbm, sub_cols), (mass_hbm, mass_ref)):
+    for source, target in ((pos_hbm, pos_ref), (dom_rows_hbm, dom_rows), (sub_rows_hbm, sub_rows),
+                           (local_cols_hbm, local_cols), (dom_cols_hbm, dom_cols), (sub_cols_hbm, sub_cols),
+                           (local_rows_hbm, local_rows), (live_hbm, live), (sub_slots_hbm, sub_slots),
+                           (dom_slots_hbm, dom_slots), (mass_hbm, mass_ref), (dom_cols_flat, dom_cols_s)):
         copy = pltpu.make_async_copy(source, target, small_sem.at[len(small)])
         copy.start()
         small.append(copy)
@@ -69,8 +72,9 @@
         h = high(value)
         return jnp.where(upper, h, value - h)
 
-    for copy in small:
-        copy.wait()
+    with jax.named_scope('small_wait'):
+        for copy in small[:3]:
+            copy.wait()
 
     for k in range(nb):
         vec[0, k] = doubled(pos_ref[:, k * tile:(k + 1) * tile])
@@ -122,18 +126,26 @@
         out = jnp.dot(jnp.concatenate([rows, rows], axis=1), weights[pair], preferred_element_type=F32)
         return out[0:8, 0:tile], out[8:16, tile:2 * tile]
 
-    def one_pair(p):
-        left, right = multiply(expanded[index[2 * p]], expanded[index[2 * p + 1]], p)
+    def block_of(t, base):
+        if base == "local":
+            return local_rows[t]
+        if base == "dom":
+            return nb + dom_slots[t - lt]
+        return nb + count_dom * width_dom + sub_slots[t - lt - ld]
+
+    def one_pair(p, base):
+        left, right = multiply(expanded[block_of(2 * p, base)], expanded[block_of(2 * p + 1, base)], p)
         both = jnp.concatenate([left, right], axis=0)
         h = both.astype(BF16)
         low = (both - h.astype(F32)).astype(BF16)
         products[pl.ds(pl.multiple_of(16 * p, 16), 16), :] = jnp.concatenate([h, low], axis=1)
-
-    def run_pairs(first, last):
+        return left, right
+
+    def run_pairs(first, last, base):
         unroll = last - first if last - first <= 24 else 16
         def body(i, carry):
             for u in range(unroll):
-                one_pair(first + i * unroll + u)
+                one_pair(first + i * unroll + u, base)
             return carry
         lax.fori_loop(0, (last - first) // unroll, body, 0)
 
@@ -152,22 +164,10 @@
             vec[k + 1, 2 * p] = left
             vec[k + 1, 2 * p + 1] = right
 
-    expand_own(0)
-
-    def fill(t, carry):
-        index[t] = local_rows[t]
-        return carry
-    lax.fori_loop(0, lt, fill, 0)
-
-    def fill_dom(t, carry):
-        index[lt + t] = nb + dom_slots[t]
-        return carry
-    lax.fori_loop(0, ld, fill_dom, 0)
-
-    def fill_sub(t, carry):
-        index[lt + ld + t] = nb + count_dom * width_dom + sub_slots[t]
-        return carry
-    lax.fori_loop(0, ls, fill_sub, 0)
+    with jax.named_scope('small_wait2'):
+        expand_own(0)
+        for copy in small[3:]:
+            copy.wait()
 
     column = 0
     for cols in (local_cols, dom_cols, sub_cols):
@@ -185,6 +185,10 @@
             place[8 * k:8 * k + 16, column:column + 8 * n] = jnp.concatenate([low, up], axis=0).astype(BF16)
         column += 8 * n
 
+    with jax.named_scope('barrier'):
+        pl.semaphore_wait(barrier, bits + count_sub - 1)
+    with jax.named_scope('exch#k=0'):
+        copies = [exchange(0)]
     used = live[0]
 
     def convert(p, masked):
@@ -205,7 +209,7 @@
                     convert(c * CHUNK // 2 + i * unroll + u, masked)
                 if multiplied:
                     for u in range(unroll):
-                        one_pair(c * CHUNK // 2 + i * unroll + u)
+                        one_pair(c * CHUNK // 2 + i * unroll + u, "local")
                 return carry
             lax.fori_loop(0, CHUNK // 2 // unroll, body, 0)
 
@@ -217,25 +221,53 @@
             vectors = {i: vec[i + 1, n] for i in {x for x, _ in sums}}
             images = {j: image[j, n] for j in {y for _, y in sums}}
             totals = [t + vectors[x] * images[y] for t, (x, y) in zip(totals, sums)]
-        return [jnp.sum(t, axis=1, keepdims=True) for t in totals]
-
-    early = [(i, j + 1) for i, j in pairs if j + 1 < ITERS] + [(i, 0) for i in range(ITERS)]
-    late = [(i, j + 1) for i, j in pairs if j + 1 == ITERS]
-
-    copies = []
+        return totals
+
+    row_of = sub8 % 4
+    lane = lax.broadcasted_iota(jnp.int32, (8, tile), 1)
+    span = tile // 4
+    last = ITERS - 1
+    order = [(i, 0) for i in range(ITERS)] + [(j, i + 1) for i, j in pairs if i < last]
+    reductions = []
+
+    def share(which, packed):
+        own[which] = jnp.sum(packed, axis=0, keepdims=True)
+        group = []
+        for o in reversed(range(1, count_dom * count_sub)):
+            target = ((a + o // count_sub) % count_dom, (b + o % count_sub) % count_sub)
+            copy = pltpu.make_async_remote_copy(
+                src_ref=own.at[which], dst_ref=sums.at[which, o - 1], send_sem=red_send.at[which, o - 1],
+                recv_sem=red_recv.at[which, o - 1], device_id=target, device_id_type=MESH)
+            copy.start()
+            group.append(copy)
+        reductions.append(group)
+
+    def shared(which):
+        for copy in reductions[which]:
+            copy.wait_recv()
+        parts = [own[which]] + [sums[which, o] for o in range(count_dom * count_sub - 1)]
+        while len(parts) > 1:
+            parts = [x + y for x, y in zip(parts[::2], parts[1::2])] + (parts[-1:] if len(parts) % 2 else [])
+        return jnp.broadcast_to(parts[0], (8, tile))
+
+    def pick(row, i):
+        mine = jnp.where(lane == span * row_of + i, row, 0.0)
+        return jnp.sum(mine, axis=1, keepdims=True) + jnp.zeros((8, tile), F32)
+
     rounds = [range(0, 0)] + [range((k - 1) * bits // ITERS, k * bits // ITERS) for k in range(1, ITERS + 1)]
     for k in range(ITERS + 1):
         if k > 0:
-            copies.append(exchange(k))
-            for j in rounds[k]:
-                pl.semaphore_signal(far_sem.at[j], inc=1, device_id=(partner_dom(j), b), device_id_type=MESH)
-            expand_own(k)
-            run_pairs(0, lt // 2)
+            with jax.named_scope(f'exch#k={k}'):
+                copies.append(exchange(k))
+                for j in rounds[k]:
+                    pl.semaphore_signal(far_sem.at[j], inc=1, device_id=(partner_dom(j), b), device_id_type=MESH)
+            with jax.named_scope(f'own#k={k}'):
+                expand_own(k)
+                run_pairs(0, lt // 2, "local")
         else:
-            pl.semaphore_wait(barrier, bits + count_sub - 1)
-            copies.append(exchange(0))
-            arrive(0, lt // 2, True, True)
-            arrive(lt // 2, lt, True, True)
+            with jax.named_scope('arrive_local'):
+                arrive(0, lt, True)
+                run_pairs(0, lt // 2, "local")
         part = scatter(0, lt)
         for n in range(nb):
             if k > 0:
@@ -243,66 +275,52 @@
             else:
                 image[k, n] = part[n]
         if k == ITERS:
-            early_sums = inner(early)
+            packed = jnp.zeros((8, tile), F32)
+            for i, total in enumerate(inner(order)):
+                value = jnp.sum(total, axis=1, keepdims=True)
+                packed = jnp.where((lane == span * row_of + i) & (sub8 < 3), value, packed)
+            share(0, packed)
         if k == 0:
-            arrive(tiles, tiles + nb)
-            arrive(lt + ld, tiles)
-            arrive(lt, lt + ld)
-        expand_received(k, copies[k])
-        run_pairs((lt + ld) // 2, tiles // 2)
-        part = scatter(lt + ld, tiles)
-        for n in range(nb):
-            image[k, n] = image[k, n] + part[n]
-        expand_received_dom(k, copies[k])
-        run_pairs(lt // 2, (lt + ld) // 2)
-        part = scatter(lt, lt + ld)
-        for n in range(nb):
-            if k > 0:
+            with jax.named_scope('arrive_rest'):
+                arrive(tiles, tiles + nb)
+                arrive(lt + ld, tiles)
+                arrive(lt, lt + ld)
+        with jax.named_scope(f'recvsub#k={k}'):
+            expand_received(k, copies[k])
+        with jax.named_scope(f'runsub#k={k}'):
+            run_pairs((lt + ld) // 2, tiles // 2, "sub")
+            part = scatter(lt + ld, tiles)
+            for n in range(nb):
                 image[k, n] = image[k, n] + part[n]
+        if k == ITERS:
+            late = jnp.where(upper, inner([(last, ITERS)])[0], 0.0)
+        with jax.named_scope(f'recvdom#k={k}'):
+            expand_received_dom(k, copies[k])
+        with jax.named_scope(f'rundom#k={k}'):
+            if k < ITERS:
+                run_pairs(lt // 2, (lt + ld) // 2, "dom")
             else:
-                image[k, n] = -(image[k, n] + part[n])
+                for p in range(lt // 2, (lt + ld) // 2):
+                    left, right = one_pair(p, "dom")
+                    late = late + left * vec[k, dom_cols_s[2 * p - lt]] + right * vec[k, dom_cols_s[2 * p + 1 - lt]]
+                value = jnp.sum(late, axis=1, keepdims=True)
+                share(1, jnp.where((lane == span * row_of) & (row_of < 3), value, 0.0))
+            part = scatter(lt, lt + ld)
+            for n in range(nb):
+                if k > 0:
+                    image[k, n] = image[k, n] + part[n]
+                else:
+                    image[k, n] = -(image[k, n] + part[n])
         if k < ITERS:
-            apply_pre(k)
-
-    totals = early_sums + inner(late)
-    order = early + late
-    lane = lax.broadcasted_iota(jnp.int32, (8, tile), 1)
-    packed = jnp.zeros((8, tile), F32)
-    for i, value in enumerate(totals):
-        packed = jnp.where(lane == i, value, packed)
-
-    own[0] = packed
-    stage_copies = []
-    for o in range(1, count_sub):
-        copy = pltpu.make_async_remote_copy(
-            src_ref=own.at[0], dst_ref=sums_sub.at[o - 1], send_sem=red_send.at[o - 1],
-            recv_sem=red_recv.at[o - 1], device_id=(a, (b + o) % count_sub), device_id_type=MESH)
-        copy.start()
-        stage_copies.append(copy)
-    for o in range(1, count_sub):
-        stage_copies[o - 1].wait_recv()
-    for o in range(1, count_sub):
-        packed = packed + sums_sub[o - 1]
-    own[1] = packed
-    for o in range(1, count_dom):
-        q = count_sub - 1 + o - 1
-        copy = pltpu.make_async_remote_copy(
-            src_ref=own.at[1], dst_ref=sums_dom.at[o - 1], send_sem=red_send.at[q],
-            recv_sem=red_recv.at[q], device_id=((a + o) % count_dom, b), device_id_type=MESH)
-        copy.start()
-        stage_copies.append(copy)
-    for o in range(1, count_dom):
-        stage_copies[count_sub - 1 + o - 1].wait_recv()
-    for o in range(1, count_dom):
-        packed = packed + sums_dom[o - 1]
-
-    def pick(i):
-        return jnp.sum(jnp.where(lane == i, packed, 0.0), axis=1, keepdims=True) + jnp.zeros((8, tile), F32)
-
+            with jax.named_scope(f'pre#k={k}'):
+                apply_pre(k)
+
+    with jax.named_scope('red0_wait'):
+        row = shared(0)
     gram = {}
-    for x, y in pairs:
-        gram[x, y] = gram[y, x] = pick(order.index((x, y + 1)))
-    first = [pick(order.index((i, 0))) for i in range(ITERS)]
+    for i, pair in enumerate(order[ITERS:]):
+        gram[pair[0], pair[1] - 1] = gram[pair[1] - 1, pair[0]] = pick(row, ITERS + i)
+    first = [pick(row, i) for i in range(ITERS)]
 
     def add(x, y):
         return y if x is None else x if y is None else x + y
@@ -314,10 +332,13 @@
         used_terms = [i for i in range(ITERS) if direction[i] is not None]
         curvature = None
         for i in used_terms:
-            inner = None
+            inner_sum = None
             for j in used_terms:
-                inner = add(inner, gram[i, j] * direction[j])
-            curvature = add(curvature, direction[i] * inner)
+                if (i, j) in gram:
+                    inner_sum = add(inner_sum, gram[i, j] * direction[j])
+            curvature = add(curvature, direction[i] * inner_sum)
+        if it == last:
+            break
         step = current / curvature
         for i in used_terms:
             coefs[i] = add(coefs[i], step * direction[i])
@@ -339,11 +360,21 @@
             current = following
 
     for n in range(nb):
-        x = vec[0, n]
-        r = image[0, n]
+        x, r, along, image_along = vec[0, n], image[0, n], None, None
         for i in range(ITERS):
-            x = x + coefs[i] * vec[i + 1, n]
-            r = r - coefs[i] * image[i + 1, n]
+            if coefs[i] is not None:
+                x = x + coefs[i] * vec[i + 1, n]
+                r = r - coefs[i] * image[i + 1, n]
+            along = add(along, direction[i] * vec[i + 1, n])
+            image_along = add(image_along, direction[i] * image[i + 1, n])
+        vec[0, n], image[0, n], vec[1, n], image[1, n] = x, r, along, image_along
+
+    with jax.named_scope('red1_wait'):
+        row = shared(1)
+    step = current / (curvature + direction[last] * direction[last] * pick(row, 0))
+    for n in range(nb):
+        x = vec[0, n] + step * vec[1, n]
+        r = image[0, n] - step * image[1, n]
         sol_ref[:, n * tile:(n + 1) * tile] = x[0:3, :]
         res_ref[:, n * tile:(n + 1) * tile] = r[0:3, :]
 
@@ -351,14 +382,17 @@
              pltpu.make_async_copy(res_ref, res_hbm, small_sem.at[1])]
     for copy in final:
         copy.start()
-    for copy in final:
-        copy.wait()
-
-    for group in copies:
+    with jax.named_scope('final_wait'):
+        for copy in final:
+            copy.wait()
+
+    with jax.named_scope('send_wait'):
+        for group in copies:
+            for copy in group:
+                copy.wait_send()
+    for group in reductions:
         for copy in group:
             copy.wait_send()
-    for copy in stage_copies:
-        copy.wait_send()
 
 
 def finish(sol_in, res_in, sol_ref, res_ref):
@@ -377,14 +411,13 @@
     width_dom = dom_rows.shape[0] // count_dom
     width_sub = sub_rows.shape[0] // count_sub
     vmem = pl.BlockSpec(memory_space=pltpu.VMEM)
-    smem = pl.BlockSpec(memory_space=pltpu.SMEM)
-    anym = pl.BlockSpec(memory_space=pl.ANY)
+    anym = pl.BlockSpec(memory_space=pltpu.HBM)
     k = ITERS + 1
-    n_red = count_sub + count_dom - 2
+    n_red = count_dom * count_sub - 1
     outs = pl.pallas_call(
         functools.partial(kernel, count_dom, count_sub, bits),
         out_shape=[jax.ShapeDtypeStruct(positions.shape, F32)] * 2,
-        in_specs=[anym, anym] + [smem] * 6 + [anym] * 7,
+        in_specs=[anym] * 16,
         out_specs=[anym, anym],
         scratch_shapes=[
             pltpu.VMEM((tiles + nb, tile, tile), F32),
@@ -394,21 +427,26 @@
             pltpu.VMEM((k, nb, 8, tile), F32),
             pltpu.VMEM((nb + count_dom * width_dom + count_sub * width_sub, 8, tile), F32),
             pltpu.VMEM((8 * tiles, 2 * tile), BF16),
-            pltpu.SMEM((tiles,), jnp.int32),
+            pltpu.SMEM(local_rows.shape, jnp.int32),
+            pltpu.SMEM(live_tiles.shape, jnp.int32),
+            pltpu.SMEM(dom_rows.shape, jnp.int32),
+            pltpu.SMEM(dom_slots.shape, jnp.int32),
+            pltpu.SMEM(sub_rows.shape, jnp.int32),
+            pltpu.SMEM(sub_slots.shape, jnp.int32),
+            pltpu.SMEM(dom_cols.shape, jnp.int32),
             pltpu.VMEM((k, bits, 3 * width_dom, tile), F32),
             pltpu.VMEM((k, bits, 3 * width_dom, tile), F32),
             pltpu.VMEM((k, count_sub - 1, 3 * width_sub, tile), F32),
             pltpu.VMEM((k, count_sub - 1, 3 * width_sub, tile), F32),
-            pltpu.VMEM((count_sub - 1, 8, tile), F32),
-            pltpu.VMEM((count_dom - 1, 8, tile), F32),
-            pltpu.VMEM((2, 8, tile), F32),
+            pltpu.VMEM((2, count_dom * count_sub - 1, 1, tile), F32),
+            pltpu.VMEM((2, 1, tile), F32),
             pltpu.SemaphoreType.DMA(((tiles + nb) // CHUNK,)),
             pltpu.SemaphoreType.DMA((k, bits)),
             pltpu.SemaphoreType.DMA((k, bits)),
             pltpu.SemaphoreType.DMA((k, count_sub - 1)),
             pltpu.SemaphoreType.DMA((k, count_sub - 1)),
-            pltpu.SemaphoreType.DMA((n_red,)),
-            pltpu.SemaphoreType.DMA((n_red,)),
+            pltpu.SemaphoreType.DMA((2, n_red)),
+            pltpu.SemaphoreType.DMA((2, n_red)),
             pltpu.VMEM(positions.shape, F32),
             pltpu.VMEM((nb, tile), F32),
             pltpu.VMEM((1, lt), jnp.int32),
@@ -416,13 +454,13 @@
             pltpu.VMEM((1, ls), jnp.int32),
             pltpu.VMEM(positions.shape, F32),
             pltpu.VMEM(positions.shape, F32),
-            pltpu.SemaphoreType.DMA((5,)),
+            pltpu.SemaphoreType.DMA((12,)),
             pltpu.SemaphoreType.REGULAR((bits,)),
         ],
         compiler_params=pltpu.CompilerParams(
             collective_id=0, has_side_effects=True, vmem_limit_bytes=60 * 1024 * 1024),
         name="fairing",
-    )(positions, mass.reshape(nb, tile), local_rows, live_tiles, dom_rows, dom_slots, sub_rows, sub_slots,
+    )(positions, mass.reshape(nb, tile), local_rows, live_tiles, dom_rows, dom_slots, sub_rows, sub_slots, dom_cols,
       local_cols.reshape(1, lt), dom_cols.reshape(1, ld), sub_cols.reshape(1, ls),
       local_tiles, dom_tiles, sub_tiles, precond)
     return pl.pallas_call(

time: 38.8 us -> 36.5 us (0.941)
  Pallas kernels: 37.3 us -> 35.1 us
    pallas_call x1, Pallas kernels: 35.7 us -> 33.5 us  [on_device(): pl.pallas_call(functools.partial(kernel, count_dom, count_sub, bits), out...]
where the time goes in v1:
time: 36.5 us; the launch traced here: 36.4 us
  Pallas kernels  35.1 us (96%)
  between operations  1.29 us (4%)
    pallas_call x1, Pallas kernels, on_device(): pl.pallas_call(functools.partial(kernel, count_dom, count_sub, bits), out...  33.5 us
    pallas_call x1, Pallas kernels, on_device(): pl.pallas_call(finish, out_shape=[jax.ShapeDtypeStruct(positions.shape, F...  1.53 us

profile of v1, /device:TPU:0, one launch (start us, length us, event | category | flops | bytes accessed | tf_op | source)
XLA Modules:
  0.0 36.4 jit_solution(13366737036583649020)
XLA Ops:
  1.3 33.5 %fairing.1 = (f32[3,4096]{1,0:T(4,128)}, f32[3,4096]{1,0:T(4,128)}) custom-call(f32[3,4096]{1,0:T(4,128)} %pos_hbm.1, f32[32,128]{1,0:T(8,128)} %bitcast.4, s32[64]{0:T(128)} %local_rows_hbm.1, s32[1]{0:T(128)S(6)} %copy.17.live_hbm, s32[256]{0:T(256)} %dom_rows_hbm.1, s32[32]{0:T(128)} %dom_slots_hbm.1, s32[64]{0:T(128)} %sub_rows_hbm.1, s32[48]{0:T(128)} %sub_slots_hbm.1, ...), custom_call_target="tpu_custom_call" | custom-call | tf_op jit(solution)/shard_map/fairing/pallas_call | solution.py:417
  34.8 1.5 %finish.1 = (f32[3,4096]{1,0:T(4,128)}, f32[3,4096]{1,0:T(4,128)}) custom-call(f32[3,4096]{1,0:T(4,128)} %get-tuple-element.4.sol_in, f32[3,4096]{1,0:T(4,128)} %get-tuple-element.5.res_in), custom_call_target="tpu_custom_call" | custom-call | tf_op jit(solution)/shard_map/finish/pallas_call | solution.py:466

commit v2 on v1

--- a/solution.py
+++ b/solution.py
@@ -19,12 +19,16 @@
     return value.astype(BF16).astype(F32)
 
 
+def drain(ref, sem):
+    pltpu.make_async_copy(ref, ref, sem).wait()
+
+
 def kernel(count_dom, count_sub, bits, pos_hbm, mass_hbm, local_rows_hbm, live_hbm, dom_rows_hbm, dom_slots_hbm,
-           sub_rows_hbm, sub_slots_hbm, dom_cols_flat, local_cols_hbm, dom_cols_hbm, sub_cols_hbm, local_hbm, dom_hbm, sub_hbm, pre_hbm, sol_hbm, res_hbm,
+           sub_rows_hbm, sub_slots_hbm, dom_cols_flat, local_cols_hbm, dom_cols_hbm, sub_cols_hbm, local_hbm, dom_hbm, sub_hbm, pre_hbm, sol_ref, res_ref,
            stage, weights, place, vec, image, expanded, products, local_rows, live, dom_rows, dom_slots, sub_rows,
            sub_slots, dom_cols_s, send_dom, recv_dom, send_sub, recv_sub,
            sums, own, load_sem, dom_send_sem, dom_recv_sem, sub_send_sem, sub_recv_sem,
-           red_send, red_recv, pos_ref, mass_ref, local_cols, dom_cols, sub_cols, sol_ref, res_ref,
+           red_send, red_recv, pos_ref, mass_ref, local_cols, dom_cols, sub_cols,
            small_sem, far_sem):
     lt, ld, ls, nb = local_hbm.shape[0], dom_hbm.shape[0], sub_hbm.shape[0], pre_hbm.shape[0]
     tile = pre_hbm.shape[1]
@@ -43,7 +47,7 @@
                            (local_cols_hbm, local_cols), (dom_cols_hbm, dom_cols), (sub_cols_hbm, sub_cols),
                            (local_rows_hbm, local_rows), (live_hbm, live), (sub_slots_hbm, sub_slots),
                            (dom_slots_hbm, dom_slots), (mass_hbm, mass_ref), (dom_cols_flat, dom_cols_s)):
-        copy = pltpu.make_async_copy(source, target, small_sem.at[len(small)])
+        copy = pltpu.make_async_copy(source, target, small_sem.at[min(len(small), 3)])
         copy.start()
         small.append(copy)
 
@@ -53,13 +57,17 @@
     for o in range(1, count_sub):
         pl.semaphore_signal(barrier, inc=1, device_id=(a, (b + o) % count_sub), device_id_type=MESH)
 
-    loads = {}
-    for start, source in ((0, local_hbm), (tiles, pre_hbm), (lt + ld, sub_hbm), (lt, dom_hbm)):
-        for first in range(0, source.shape[0], CHUNK):
-            copy = pltpu.make_async_copy(source.at[pl.ds(first, CHUNK)], stage.at[pl.ds(start + first, CHUNK)],
-                                         load_sem.at[(start + first) // CHUNK])
-            copy.start()
-            loads[(start + first) // CHUNK] = copy
+    groups = ((0, 2 * CHUNK), (2 * CHUNK, lt), (lt + ld, tiles), (lt, lt + ld), (tiles, tiles + nb))
+    sources = (local_hbm, local_hbm, sub_hbm, dom_hbm, pre_hbm)
+    for g, ((first, end), source) in enumerate(zip(groups, sources)):
+        offset = first if g < 2 else 0
+        for c in range(0, end - first, CHUNK):
+            pltpu.make_async_copy(source.at[pl.ds(offset + c, CHUNK)], stage.at[pl.ds(first + c, CHUNK)],
+                                  load_sem.at[g]).start()
+
+    def loaded(g):
+        first, end = groups[g]
+        drain(stage.at[pl.ds(first, end - first)], load_sem.at[g])
 
     sub8 = lax.broadcasted_iota(jnp.int32, (8, tile), 0)
     upper = sub8 < 4
@@ -80,25 +88,25 @@
         vec[0, k] = doubled(pos_ref[:, k * tile:(k + 1) * tile])
 
     def exchange(k):
-        copies = []
+        copies = {}
+        for o in sorted(range(1, count_sub), key=lambda o: abs(2 * o - count_sub)):
+            other = (b + o) % count_sub
+            for s in range(width_sub):
+                send_sub[k, o - 1, 3 * s:3 * s + 3, :] = vec[k, sub_rows[other * width_sub + s], 0:3, :]
+            copy = pltpu.make_async_remote_copy(
+                src_ref=send_sub.at[k, o - 1], dst_ref=recv_sub.at[k, o - 1], send_sem=sub_send_sem,
+                recv_sem=sub_recv_sem.at[k % 2, o - 1], device_id=(a, other), device_id_type=MESH)
+            copy.start()
+            copies["sub", o] = copy
         for j in reversed(range(bits)):
             other = partner_dom(j)
             for s in range(width_dom):
                 send_dom[k, j, 3 * s:3 * s + 3, :] = vec[k, dom_rows[other * width_dom + s], 0:3, :]
             copy = pltpu.make_async_remote_copy(
-                src_ref=send_dom.at[k, j], dst_ref=recv_dom.at[k, j], send_sem=dom_send_sem.at[k, j],
-                recv_sem=dom_recv_sem.at[k, j], device_id=(other, b), device_id_type=MESH)
+                src_ref=send_dom.at[k, j], dst_ref=recv_dom.at[k, j], send_sem=dom_send_sem,
+                recv_sem=dom_recv_sem.at[k % 2, j], device_id=(other, b), device_id_type=MESH)
             copy.start()
-            copies.append(copy)
-        for o in range(1, count_sub):
-            other = (b + o) % count_sub
-            for s in range(width_sub):
-                send_sub[k, o - 1, 3 * s:3 * s + 3, :] = vec[k, sub_rows[other * width_sub + s], 0:3, :]
-            copy = pltpu.make_async_remote_copy(
-                src_ref=send_sub.at[k, o - 1], dst_ref=recv_sub.at[k, o - 1], send_sem=sub_send_sem.at[k, o - 1],
-                recv_sem=sub_recv_sem.at[k, o - 1], device_id=(a, other), device_id_type=MESH)
-            copy.start()
-            copies.append(copy)
+            copies["dom", j] = copy
         return copies
 
     def expand_own(k):
@@ -107,7 +115,7 @@
 
     def expand_received(k, copies):
         for o in range(1, count_sub):
-            copies[bits + o - 1].wait_recv()
+            copies["sub", o].wait_recv()
             base = nb + count_dom * width_dom + ((b + count_sub - o) % count_sub) * width_sub
             for s in range(width_sub):
                 expanded[base + s] = split_rows(doubled(recv_sub[k, o - 1, 3 * s:3 * s + 3, :]))
@@ -116,7 +124,7 @@
         for j in rounds[k]:
             pl.semaphore_wait(far_sem.at[j], 1)
         for j in range(bits):
-            copies[bits - 1 - j].wait_recv()
+            copies["dom", j].wait_recv()
             base = nb + partner_dom(j) * width_dom
             for s in range(width_dom):
                 expanded[base + s] = split_rows(doubled(recv_dom[k, j, 3 * s:3 * s + 3, :]))
@@ -142,12 +150,8 @@
         return left, right
 
     def run_pairs(first, last, base):
-        unroll = last - first if last - first <= 24 else 16
-        def body(i, carry):
-            for u in range(unroll):
-                one_pair(first + i * unroll + u, base)
-            return carry
-        lax.fori_loop(0, (last - first) // unroll, body, 0)
+        for p in range(first, last):
+            one_pair(p, base)
 
     def scatter(first, last):
         out = jnp.dot(place[:, 8 * first:8 * last], products[8 * first:8 * last, :], preferred_element_type=F32)
@@ -200,18 +204,14 @@
             weights[p, 0:tile, side * tile:(side + 1) * tile] = h
             weights[p, tile:2 * tile, side * tile:(side + 1) * tile] = (value - h.astype(F32)).astype(BF16)
 
-    def arrive(first, last, masked=False, multiplied=False, unroll=4):
-        for c in range(first // CHUNK, last // CHUNK):
-            loads[c].wait()
-
-            def body(i, carry):
-                for u in range(unroll):
-                    convert(c * CHUNK // 2 + i * unroll + u, masked)
-                if multiplied:
-                    for u in range(unroll):
-                        one_pair(c * CHUNK // 2 + i * unroll + u, "local")
-                return carry
-            lax.fori_loop(0, CHUNK // 2 // unroll, body, 0)
+    def convert_group(g, masked=False):
+        first, end = groups[g]
+
+        def body(i, carry):
+            for u in range(8):
+                convert(first // 2 + i * 8 + u, masked)
+            return carry
+        lax.fori_loop(0, (end - first) // 16, body, 0)
 
     pairs = [(i, j) for i in range(ITERS) for j in range(i, ITERS)]
 
@@ -228,23 +228,18 @@
     span = tile // 4
     last = ITERS - 1
     order = [(i, 0) for i in range(ITERS)] + [(j, i + 1) for i, j in pairs if i < last]
-    reductions = []
 
     def share(which, packed):
         own[which] = jnp.sum(packed, axis=0, keepdims=True)
-        group = []
         for o in reversed(range(1, count_dom * count_sub)):
             target = ((a + o // count_sub) % count_dom, (b + o % count_sub) % count_sub)
             copy = pltpu.make_async_remote_copy(
-                src_ref=own.at[which], dst_ref=sums.at[which, o - 1], send_sem=red_send.at[which, o - 1],
-                recv_sem=red_recv.at[which, o - 1], device_id=target, device_id_type=MESH)
+                src_ref=own.at[which], dst_ref=sums.at[which, o - 1], send_sem=red_send,
+                recv_sem=red_recv.at[which], device_id=target, device_id_type=MESH)
             copy.start()
-            group.append(copy)
-        reductions.append(group)
 
     def shared(which):
-        for copy in reductions[which]:
-            copy.wait_recv()
+        drain(sums.at[which], red_recv.at[which])
         parts = [own[which]] + [sums[which, o] for o in range(count_dom * count_sub - 1)]
         while len(parts) > 1:
             parts = [x + y for x, y in zip(parts[::2], parts[1::2])] + (parts[-1:] if len(parts) % 2 else [])
@@ -266,8 +261,14 @@
                 run_pairs(0, lt // 2, "local")
         else:
             with jax.named_scope('arrive_local'):
-                arrive(0, lt, True)
+                loaded(0)
+                convert_group(0, True)
+                loaded(1)
+                convert_group(1, True)
+                loaded(2)
                 run_pairs(0, lt // 2, "local")
+                for p in range((lt + ld) // 2, tiles // 2):
+                    convert(p, False)
         part = scatter(0, lt)
         for n in range(nb):
             if k > 0:
@@ -282,9 +283,10 @@
             share(0, packed)
         if k == 0:
             with jax.named_scope('arrive_rest'):
-                arrive(tiles, tiles + nb)
-                arrive(lt + ld, tiles)
-                arrive(lt, lt + ld)
+                loaded(3)
+                convert_group(3)
+                loaded(4)
+                convert_group(4)
         with jax.named_scope(f'recvsub#k={k}'):
             expand_received(k, copies[k])
         with jax.named_scope(f'runsub#k={k}'):
@@ -378,21 +380,10 @@
         sol_ref[:, n * tile:(n + 1) * tile] = x[0:3, :]
         res_ref[:, n * tile:(n + 1) * tile] = r[0:3, :]
 
-    final = [pltpu.make_async_copy(sol_ref, sol_hbm, small_sem.at[0]),
-             pltpu.make_async_copy(res_ref, res_hbm, small_sem.at[1])]
-    for copy in final:
-        copy.start()
-    with jax.named_scope('final_wait'):
-        for copy in final:
-            copy.wait()
-
     with jax.named_scope('send_wait'):
-        for group in copies:
-            for copy in group:
-                copy.wait_send()
-    for group in reductions:
-        for copy in group:
-            copy.wait_send()
+        drain(send_sub, sub_send_sem)
+        drain(send_dom, dom_send_sem)
+        drain(sums, red_send)
 
 
 def finish(sol_in, res_in, sol_ref, res_ref):
@@ -416,9 +407,9 @@
     n_red = count_dom * count_sub - 1
     outs = pl.pallas_call(
         functools.partial(kernel, count_dom, count_sub, bits),
-        out_shape=[jax.ShapeDtypeStruct(positions.shape, F32)] * 2,
+        out_shape=[pltpu.VMEM(positions.shape, F32)] * 2,
         in_specs=[anym] * 16,
-        out_specs=[anym, anym],
+        out_specs=[vmem, vmem],
         scratch_shapes=[
             pltpu.VMEM((tiles + nb, tile, tile), F32),
             pltpu.VMEM(((tiles + nb) // 2, 2 * tile, 2 * tile), BF16),
@@ -440,25 +431,23 @@
             pltpu.VMEM((k, count_sub - 1, 3 * width_sub, tile), F32),
             pltpu.VMEM((2, count_dom * count_sub - 1, 1, tile), F32),
             pltpu.VMEM((2, 1, tile), F32),
-            pltpu.SemaphoreType.DMA(((tiles + nb) // CHUNK,)),
-            pltpu.SemaphoreType.DMA((k, bits)),
-            pltpu.SemaphoreType.DMA((k, bits)),
-            pltpu.SemaphoreType.DMA((k, count_sub - 1)),
-            pltpu.SemaphoreType.DMA((k, count_sub - 1)),
-            pltpu.SemaphoreType.DMA((2, n_red)),
-            pltpu.SemaphoreType.DMA((2, n_red)),
+            pltpu.SemaphoreType.DMA((5,)),
+            pltpu.SemaphoreType.DMA,
+            pltpu.SemaphoreType.DMA((2, bits)),
+            pltpu.SemaphoreType.DMA,
+            pltpu.SemaphoreType.DMA((2, count_sub - 1)),
+            pltpu.SemaphoreType.DMA,
+            pltpu.SemaphoreType.DMA((2,)),
             pltpu.VMEM(positions.shape, F32),
             pltpu.VMEM((nb, tile), F32),
             pltpu.VMEM((1, lt), jnp.int32),
             pltpu.VMEM((1, ld), jnp.int32),
             pltpu.VMEM((1, ls), jnp.int32),
-            pltpu.VMEM(positions.shape, F32),
-            pltpu.VMEM(positions.shape, F32),
-            pltpu.SemaphoreType.DMA((12,)),
+            pltpu.SemaphoreType.DMA((4,)),
             pltpu.SemaphoreType.REGULAR((bits,)),
         ],
         compiler_params=pltpu.CompilerParams(
-            collective_id=0, has_side_effects=True, vmem_limit_bytes=60 * 1024 * 1024),
+            collective_id=0, has_side_effects=True, vmem_limit_bytes=62914560),
         name="fairing",
     )(positions, mass.reshape(nb, tile), local_rows, live_tiles, dom_rows, dom_slots, sub_rows, sub_slots, dom_cols,
       local_cols.reshape(1, lt), dom_cols.reshape(1, ld), sub_cols.reshape(1, ls),
@@ -468,6 +457,7 @@
         out_shape=[jax.ShapeDtypeStruct(positions.shape, F32)] * 2,
         in_specs=[vmem, vmem],
         out_specs=[vmem, vmem],
+        compiler_params=pltpu.CompilerParams(vmem_limit_bytes=8388608),
         name="finish",
     )(*outs)
 

time: 36.5 us -> 32.7 us (0.90)
  Pallas kernels: 35.1 us -> 31.2 us
    pallas_call x1, Pallas kernels: 33.5 us -> 30.6 us  [on_device(): pl.pallas_call(functools.partial(kernel, count_dom, count_sub, bits), out...]
    pallas_call x1, Pallas kernels: 1.53 us -> 0.66 us  [on_device(): pl.pallas_call(finish, out_shape=[jax.ShapeDtypeStruct(positions.shape, F...]
where the time goes in v2:
time: 32.7 us; the launch traced here: 32.5 us
  Pallas kernels  31.2 us (95%)
  between operations  1.29 us (4%)
    pallas_call x1, Pallas kernels, on_device(): pl.pallas_call(functools.partial(kernel, count_dom, count_sub, bits), out...  30.6 us
    pallas_call x1, Pallas kernels, on_device(): pl.pallas_call(finish, out_shape=[jax.ShapeDtypeStruct(positions.shape, F...  0.66 us

profile of v2, /device:TPU:0, one launch (start us, length us, event | category | flops | bytes accessed | tf_op | source)
XLA Modules:
  0.0 32.5 jit_solution(3720502651474271268)
XLA Ops:
  1.3 30.6 %fairing.1 = (f32[3,4096]{1,0:T(4,128)S(1)}, f32[3,4096]{1,0:T(4,128)S(1)}) custom-call(f32[3,4096]{1,0:T(4,128)} %pos_hbm.1, f32[32,128]{1,0:T(8,128)} %bitcast.4, s32[64]{0:T(128)} %local_rows_hbm.1, s32[1]{0:T(128)S(6)} %copy.17.live_hbm, s32[256]{0:T(256)} %dom_rows_hbm.1, s32[32]{0:T(128)} %dom_slots_hbm.1, s32[64]{0:T(128)} %sub_rows_hbm.1, ...), custom_call_target="tpu_custom_call" | custom-call | tf_op jit(solution)/shard_map/fairing/pallas_call | solution.py:408
  31.9 0.7 %finish.1 = (f32[3,4096]{1,0:T(4,128)}, f32[3,4096]{1,0:T(4,128)}) custom-call(f32[3,4096]{1,0:T(4,128)S(1)} %get-tuple-element.4.sol_in, f32[3,4096]{1,0:T(4,128)S(1)} %get-tuple-element.5.res_in), custom_call_target="tpu_custom_call" | custom-call | tf_op jit(solution)/shard_map/finish/pallas_call | solution.py:455

commit v3 on v2

--- a/solution.py
+++ b/solution.py
@@ -24,12 +24,12 @@
 
 
 def kernel(count_dom, count_sub, bits, pos_hbm, mass_hbm, local_rows_hbm, live_hbm, dom_rows_hbm, dom_slots_hbm,
-           sub_rows_hbm, sub_slots_hbm, dom_cols_flat, local_cols_hbm, dom_cols_hbm, sub_cols_hbm, local_hbm, dom_hbm, sub_hbm, pre_hbm, sol_ref, res_ref,
+           sub_rows_hbm, sub_slots_hbm, dom_cols_flat, sub_cols_flat, local_cols_hbm, dom_cols_hbm, sub_cols_hbm, local_hbm, dom_hbm, sub_hbm, pre_hbm, sol_ref, res_ref,
            stage, weights, place, vec, image, expanded, products, local_rows, live, dom_rows, dom_slots, sub_rows,
-           sub_slots, dom_cols_s, send_dom, recv_dom, send_sub, recv_sub,
+           sub_slots, dom_cols_s, sub_cols_s, send_dom, recv_dom, send_sub, recv_sub,
            sums, own, load_sem, dom_send_sem, dom_recv_sem, sub_send_sem, sub_recv_sem,
            red_send, red_recv, pos_ref, mass_ref, local_cols, dom_cols, sub_cols,
-           small_sem, far_sem):
+           small_sem, far_sem, fused, blocks):
     lt, ld, ls, nb = local_hbm.shape[0], dom_hbm.shape[0], sub_hbm.shape[0], pre_hbm.shape[0]
     tile = pre_hbm.shape[1]
     width_dom = dom_rows_hbm.shape[0] // count_dom
@@ -46,13 +46,13 @@
     for source, target in ((pos_hbm, pos_ref), (dom_rows_hbm, dom_rows), (sub_rows_hbm, sub_rows),
                            (local_cols_hbm, local_cols), (dom_cols_hbm, dom_cols), (sub_cols_hbm, sub_cols),
                            (local_rows_hbm, local_rows), (live_hbm, live), (sub_slots_hbm, sub_slots),
-                           (dom_slots_hbm, dom_slots), (mass_hbm, mass_ref), (dom_cols_flat, dom_cols_s)):
+                           (dom_slots_hbm, dom_slots), (mass_hbm, mass_ref), (dom_cols_flat, dom_cols_s), (sub_cols_flat, sub_cols_s)):
         copy = pltpu.make_async_copy(source, target, small_sem.at[min(len(small), 3)])
         copy.start()
         small.append(copy)
 
     barrier = pltpu.get_barrier_semaphore()
-    for j in range(bits):
+    for j in reversed(range(bits)):
         pl.semaphore_signal(barrier, inc=1, device_id=(partner_dom(j), b), device_id_type=MESH)
     for o in range(1, count_sub):
         pl.semaphore_signal(barrier, inc=1, device_id=(a, (b + o) % count_sub), device_id_type=MESH)
@@ -89,6 +89,15 @@
 
     def exchange(k):
         copies = {}
+        for j in [bits - 1]:
+            other = partner_dom(j)
+            for s in range(width_dom):
+                send_dom[k, j, 3 * s:3 * s + 3, :] = vec[k, dom_rows[other * width_dom + s], 0:3, :]
+            copy = pltpu.make_async_remote_copy(
+                src_ref=send_dom.at[k, j], dst_ref=recv_dom.at[k, j], send_sem=dom_send_sem,
+                recv_sem=dom_recv_sem.at[k % 2, j], device_id=(other, b), device_id_type=MESH)
+            copy.start()
+            copies["dom", j] = copy
         for o in sorted(range(1, count_sub), key=lambda o: abs(2 * o - count_sub)):
             other = (b + o) % count_sub
             for s in range(width_sub):
@@ -98,7 +107,7 @@
                 recv_sem=sub_recv_sem.at[k % 2, o - 1], device_id=(a, other), device_id_type=MESH)
             copy.start()
             copies["sub", o] = copy
-        for j in reversed(range(bits)):
+        for j in reversed(range(bits - 1)):
             other = partner_dom(j)
             for s in range(width_dom):
                 send_dom[k, j, 3 * s:3 * s + 3, :] = vec[k, dom_rows[other * width_dom + s], 0:3, :]
@@ -129,9 +138,9 @@
             for s in range(width_dom):
                 expanded[base + s] = split_rows(doubled(recv_dom[k, j, 3 * s:3 * s + 3, :]))
 
-    def multiply(left, right, pair):
+    def multiply(left, right, matrix):
         rows = jnp.concatenate([left, right], axis=0).astype(BF16)
-        out = jnp.dot(jnp.concatenate([rows, rows], axis=1), weights[pair], preferred_element_type=F32)
+        out = jnp.dot(jnp.concatenate([rows, rows], axis=1), matrix, preferred_element_type=F32)
         return out[0:8, 0:tile], out[8:16, tile:2 * tile]
 
     def block_of(t, base):
@@ -141,8 +150,9 @@
             return nb + dom_slots[t - lt]
         return nb + count_dom * width_dom + sub_slots[t - lt - ld]
 
-    def one_pair(p, base):
-        left, right = multiply(expanded[block_of(2 * p, base)], expanded[block_of(2 * p + 1, base)], p)
+    def one_pair(p, base, matrix=None):
+        left, right = multiply(expanded[block_of(2 * p, base)], expanded[block_of(2 * p + 1, base)],
+                               weights[p] if matrix is None else matrix)
         both = jnp.concatenate([left, right], axis=0)
         h = both.astype(BF16)
         low = (both - h.astype(F32)).astype(BF16)
@@ -159,7 +169,8 @@
 
     def apply_pre(k):
         for p in range(nb // 2):
-            left, right = multiply(split_rows(image[k, 2 * p]), split_rows(image[k, 2 * p + 1]), tiles // 2 + p)
+            left, right = multiply(split_rows(image[k, 2 * p]), split_rows(image[k, 2 * p + 1]),
+                                   jnp.concatenate([blocks[2 * p], blocks[2 * p + 1]], axis=1))
             left = left + pltpu.roll(left, 4, 0)
             right = right + pltpu.roll(right, 4, 0)
             if k > 0:
@@ -195,7 +206,7 @@
         copies = [exchange(0)]
     used = live[0]
 
-    def convert(p, masked):
+    def convert(p, masked=False):
         for side in range(2):
             value = stage[2 * p + side]
             if masked:
@@ -212,6 +223,48 @@
                 convert(first // 2 + i * 8 + u, masked)
             return carry
         lax.fori_loop(0, (end - first) // 16, body, 0)
+
+    def convert_blocks():
+        def body(i, carry):
+            for u in range(16):
+                value = stage[tiles + i * 16 + u]
+                h = value.astype(BF16)
+                blocks[i * 16 + u, 0:tile] = h
+                blocks[i * 16 + u, tile:2 * tile] = (value - h.astype(F32)).astype(BF16)
+            return carry
+        lax.fori_loop(0, nb // 16, body, 0)
+
+    def fuse(t):
+        side = slice(t % 2 * tile, t % 2 * tile + tile)
+        block = blocks[dom_cols_s[t]]
+        high_part = weights[(lt + t) // 2, 0:tile, side]
+        low_part = weights[(lt + t) // 2, tile:2 * tile, side]
+        value = (jnp.dot(jnp.concatenate([high_part, high_part], axis=1), block, preferred_element_type=F32)
+                 + jnp.dot(low_part, block[0:tile], preferred_element_type=F32))
+        h = value.astype(BF16)
+        fused[t // 2, 0:tile, side] = h
+        fused[t // 2, tile:2 * tile, side] = (value - h.astype(F32)).astype(BF16)
+
+    def meet(total, first, last, base, cols):
+        for p in range(first, last):
+            left, right = one_pair(p, base)
+            total = (total + left * vec[ITERS, cols[2 * (p - first)]]
+                     + right * vec[ITERS, cols[2 * (p - first) + 1]])
+        return total
+
+    def add_parts(k, first, last):
+        part = scatter(first, last)
+        for n in range(nb):
+            image[k, n] = image[k, n] + part[n]
+
+    def run_fused():
+        for p in range(ld // 2):
+            one_pair(lt // 2 + p, "dom", fused[p])
+
+    def add_fused(k):
+        part = scatter(lt, lt + ld)
+        for n in range(nb):
+            vec[k + 1, n] = vec[k + 1, n] + part[n]
 
     pairs = [(i, j) for i in range(ITERS) for j in range(i, ITERS)]
 
@@ -258,7 +311,11 @@
                     pl.semaphore_signal(far_sem.at[j], inc=1, device_id=(partner_dom(j), b), device_id_type=MESH)
             with jax.named_scope(f'own#k={k}'):
                 expand_own(k)
+                if k > 1:
+                    run_pairs(lt // 2, (lt + ld) // 2, "dom")
                 run_pairs(0, lt // 2, "local")
+                if k > 1:
+                    add_parts(k - 1, lt, lt + ld)
         else:
             with jax.named_scope('arrive_local'):
                 loaded(0)
@@ -268,7 +325,7 @@
                 loaded(2)
                 run_pairs(0, lt // 2, "local")
                 for p in range((lt + ld) // 2, tiles // 2):
-                    convert(p, False)
+                    convert(p)
         part = scatter(0, lt)
         for n in range(nb):
             if k > 0:
@@ -281,41 +338,61 @@
                 value = jnp.sum(total, axis=1, keepdims=True)
                 packed = jnp.where((lane == span * row_of + i) & (sub8 < 3), value, packed)
             share(0, packed)
+        if k == 1 and ITERS > 1:
+            with jax.named_scope('fuse'):
+                for t in range(ld):
+                    fuse(t)
         if k == 0:
             with jax.named_scope('arrive_rest'):
                 loaded(3)
                 convert_group(3)
                 loaded(4)
-                convert_group(4)
+                convert_blocks()
+        if k == ITERS:
+            late = jnp.where(upper, inner([(last, ITERS)])[0], 0.0)
         with jax.named_scope(f'recvsub#k={k}'):
             expand_received(k, copies[k])
         with jax.named_scope(f'runsub#k={k}'):
-            run_pairs((lt + ld) // 2, tiles // 2, "sub")
-            part = scatter(lt + ld, tiles)
-            for n in range(nb):
-                image[k, n] = image[k, n] + part[n]
-        if k == ITERS:
-            late = jnp.where(upper, inner([(last, ITERS)])[0], 0.0)
+            if k == ITERS:
+                late = meet(late, (lt + ld) // 2, tiles // 2, "sub", sub_cols_s)
+            else:
+                run_pairs((lt + ld) // 2, tiles // 2, "sub")
+        if 0 < k < ITERS:
+            @pl.when(b % 2 == 0)
+            def _(k=k):
+                with jax.named_scope(f'pre#k={k}'):
+                    add_parts(k, lt + ld, tiles)
+                    apply_pre(k)
+                with jax.named_scope(f'recvdom#k={k}'):
+                    expand_received_dom(k, copies[k])
+                with jax.named_scope(f'rundom#k={k}'):
+                    run_fused()
+                    add_fused(k)
+
+            @pl.when(b % 2 == 1)
+            def _(k=k):
+                with jax.named_scope(f'recvdom#k={k}'):
+                    expand_received_dom(k, copies[k])
+                with jax.named_scope(f'rundom#k={k}'):
+                    run_fused()
+                    add_parts(k, lt + ld, tiles)
+                    apply_pre(k)
+                    add_fused(k)
+            continue
         with jax.named_scope(f'recvdom#k={k}'):
             expand_received_dom(k, copies[k])
         with jax.named_scope(f'rundom#k={k}'):
-            if k < ITERS:
+            if k == 0:
                 run_pairs(lt // 2, (lt + ld) // 2, "dom")
+                part = scatter(lt, tiles)
+                for n in range(nb):
+                    image[k, n] = -(image[k, n] + part[n])
+                apply_pre(k)
             else:
-                for p in range(lt // 2, (lt + ld) // 2):
-                    left, right = one_pair(p, "dom")
-                    late = late + left * vec[k, dom_cols_s[2 * p - lt]] + right * vec[k, dom_cols_s[2 * p + 1 - lt]]
+                late = meet(late, lt // 2, (lt + ld) // 2, "dom", dom_cols_s)
                 value = jnp.sum(late, axis=1, keepdims=True)
                 share(1, jnp.where((lane == span * row_of) & (row_of < 3), value, 0.0))
-            part = scatter(lt, lt + ld)
-            for n in range(nb):
-                if k > 0:
-                    image[k, n] = image[k, n] + part[n]
-                else:
-                    image[k, n] = -(image[k, n] + part[n])
-        if k < ITERS:
-            with jax.named_scope(f'pre#k={k}'):
-                apply_pre(k)
+                add_parts(k, lt, tiles)
 
     with jax.named_scope('red0_wait'):
         row = shared(0)
@@ -408,11 +485,11 @@
     outs = pl.pallas_call(
         functools.partial(kernel, count_dom, count_sub, bits),
         out_shape=[pltpu.VMEM(positions.shape, F32)] * 2,
-        in_specs=[anym] * 16,
+        in_specs=[anym] * 17,
         out_specs=[vmem, vmem],
         scratch_shapes=[
             pltpu.VMEM((tiles + nb, tile, tile), F32),
-            pltpu.VMEM(((tiles + nb) // 2, 2 * tile, 2 * tile), BF16),
+            pltpu.VMEM((tiles // 2, 2 * tile, 2 * tile), BF16),
             pltpu.VMEM((8 * nb, 8 * tiles), BF16),
             pltpu.VMEM((k, nb, 8, tile), F32),
             pltpu.VMEM((k, nb, 8, tile), F32),
@@ -425,6 +502,7 @@
             pltpu.SMEM(sub_rows.shape, jnp.int32),
             pltpu.SMEM(sub_slots.shape, jnp.int32),
             pltpu.SMEM(dom_cols.shape, jnp.int32),
+            pltpu.SMEM(sub_cols.shape, jnp.int32),
             pltpu.VMEM((k, bits, 3 * width_dom, tile), F32),
             pltpu.VMEM((k, bits, 3 * width_dom, tile), F32),
             pltpu.VMEM((k, count_sub - 1, 3 * width_sub, tile), F32),
@@ -445,11 +523,13 @@
             pltpu.VMEM((1, ls), jnp.int32),
             pltpu.SemaphoreType.DMA((4,)),
             pltpu.SemaphoreType.REGULAR((bits,)),
+            pltpu.VMEM((ld // 2, 2 * tile, 2 * tile), BF16),
+            pltpu.VMEM((nb, 2 * tile, tile), BF16),
         ],
         compiler_params=pltpu.CompilerParams(
             collective_id=0, has_side_effects=True, vmem_limit_bytes=62914560),
         name="fairing",
-    )(positions, mass.reshape(nb, tile), local_rows, live_tiles, dom_rows, dom_slots, sub_rows, sub_slots, dom_cols,
+    )(positions, mass.reshape(nb, tile), local_rows, live_tiles, dom_rows, dom_slots, sub_rows, sub_slots, dom_cols, sub_cols,
       local_cols.reshape(1, lt), dom_cols.reshape(1, ld), sub_cols.reshape(1, ls),
       local_tiles, dom_tiles, sub_tiles, precond)
     return pl.pallas_call(

time: 32.7 us -> 32.2 us (0.985)
  Pallas kernels: 31.2 us -> 30.8 us
    pallas_call x1, Pallas kernels: 30.6 us -> 30.1 us  [on_device(): pl.pallas_call(functools.partial(kernel, count_dom, count_sub, bits), out...]
where the time goes in v3:
time: 32.2 us; the launch traced here: 32.1 us
  Pallas kernels  30.8 us (96%)
  between operations  1.29 us (4%)
    pallas_call x1, Pallas kernels, on_device(): pl.pallas_call(functools.partial(kernel, count_dom, count_sub, bits), out...  30.1 us
    pallas_call x1, Pallas kernels, on_device(): pl.pallas_call(finish, out_shape=[jax.ShapeDtypeStruct(positions.shape, F...  0.66 us

profile of v3, /device:TPU:0, one launch (start us, length us, event | category | flops | bytes accessed | tf_op | source)
XLA Modules:
  0.0 32.1 jit_solution(13927940874952293427)
XLA Ops:
  1.3 30.1 %fairing.1 = (f32[3,4096]{1,0:T(4,128)S(1)}, f32[3,4096]{1,0:T(4,128)S(1)}) custom-call(f32[3,4096]{1,0:T(4,128)} %pos_hbm.1, f32[32,128]{1,0:T(8,128)} %bitcast.4, s32[64]{0:T(128)} %local_rows_hbm.1, s32[1]{0:T(128)S(6)} %copy.17.live_hbm, s32[256]{0:T(256)} %dom_rows_hbm.1, s32[32]{0:T(128)} %dom_slots_hbm.1, s32[64]{0:T(128)} %sub_rows_hbm.1, ...), custom_call_target="tpu_custom_call" | custom-call | tf_op jit(solution)/shard_map/fairing/pallas_call | solution.py:485
  31.4 0.7 %finish.1 = (f32[3,4096]{1,0:T(4,128)}, f32[3,4096]{1,0:T(4,128)}) custom-call(f32[3,4096]{1,0:T(4,128)S(1)} %get-tuple-element.4.sol_in, f32[3,4096]{1,0:T(4,128)S(1)} %get-tuple-element.5.res_in), custom_call_target="tpu_custom_call" | custom-call | tf_op jit(solution)/shard_map/finish/pallas_call | solution.py:535

commit v4 on v3

--- a/solution.py
+++ b/solution.py
@@ -193,10 +193,12 @@
                          preferred_element_type=F32)
         pattern = ((lax.broadcasted_iota(jnp.int32, (8, 8 * n), 1) % 4)
                    == (lax.broadcasted_iota(jnp.int32, (8, 8 * n), 0) % 4))
+        if column == 0:
+            pattern = pattern & (lax.broadcasted_iota(jnp.int32, (8, 8 * n), 1) < 8 * live[0])
         spread = jnp.where(pattern, spread, -1.0)
         for k in range(0, nb, 2):
-            low = jnp.where(jnp.abs(spread - k) < 0.5, 1.0, 0.0)
-            up = jnp.where(jnp.abs(spread - (k + 1)) < 0.5, 1.0, 0.0)
+            low = jnp.where(spread == k, 1.0, 0.0)
+            up = jnp.where(spread == k + 1, 1.0, 0.0)
             place[8 * k:8 * k + 16, column:column + 8 * n] = jnp.concatenate([low, up], axis=0).astype(BF16)
         column += 8 * n
 
@@ -204,23 +206,19 @@
         pl.semaphore_wait(barrier, bits + count_sub - 1)
     with jax.named_scope('exch#k=0'):
         copies = [exchange(0)]
-    used = live[0]
-
-    def convert(p, masked=False):
+    def convert(p):
         for side in range(2):
             value = stage[2 * p + side]
-            if masked:
-                value = value * (2 * p + side < used).astype(F32)
             h = value.astype(BF16)
             weights[p, 0:tile, side * tile:(side + 1) * tile] = h
             weights[p, tile:2 * tile, side * tile:(side + 1) * tile] = (value - h.astype(F32)).astype(BF16)
 
-    def convert_group(g, masked=False):
+    def convert_group(g):
         first, end = groups[g]
 
         def body(i, carry):
             for u in range(8):
-                convert(first // 2 + i * 8 + u, masked)
+                convert(first // 2 + i * 8 + u)
             return carry
         lax.fori_loop(0, (end - first) // 16, body, 0)
 
@@ -319,9 +317,9 @@
         else:
             with jax.named_scope('arrive_local'):
                 loaded(0)
-                convert_group(0, True)
+                convert_group(0)
                 loaded(1)
-                convert_group(1, True)
+                convert_group(1)
                 loaded(2)
                 run_pairs(0, lt // 2, "local")
                 for p in range((lt + ld) // 2, tiles // 2):

time: 32.2 us -> 32.3 us (level)
  no operation moved by 1% of the time
where the time goes in v4:
time: 32.3 us; the launch traced here: 32.1 us
  Pallas kernels  30.8 us (95%)
  between operations  1.29 us (4%)
    pallas_call x1, Pallas kernels, on_device(): pl.pallas_call(functools.partial(kernel, count_dom, count_sub, bits), out...  30.1 us
    pallas_call x1, Pallas kernels, on_device(): pl.pallas_call(finish, out_shape=[jax.ShapeDtypeStruct(positions.shape, F...  0.66 us

profile of v4, /device:TPU:0, one launch (start us, length us, event | category | flops | bytes accessed | tf_op | source)
XLA Modules:
  0.0 32.1 jit_solution(1599391057499140950)
XLA Ops:
  1.3 30.1 %fairing.1 = (f32[3,4096]{1,0:T(4,128)S(1)}, f32[3,4096]{1,0:T(4,128)S(1)}) custom-call(f32[3,4096]{1,0:T(4,128)} %pos_hbm.1, f32[32,128]{1,0:T(8,128)} %bitcast.4, s32[64]{0:T(128)} %local_rows_hbm.1, s32[1]{0:T(128)S(6)} %copy.17.live_hbm, s32[256]{0:T(256)} %dom_rows_hbm.1, s32[32]{0:T(128)} %dom_slots_hbm.1, s32[64]{0:T(128)} %sub_rows_hbm.1, ...), custom_call_target="tpu_custom_call" | custom-call | tf_op jit(solution)/shard_map/fairing/pallas_call | solution.py:483
  31.4 0.7 %finish.1 = (f32[3,4096]{1,0:T(4,128)}, f32[3,4096]{1,0:T(4,128)}) custom-call(f32[3,4096]{1,0:T(4,128)S(1)} %get-tuple-element.4.sol_in, f32[3,4096]{1,0:T(4,128)S(1)} %get-tuple-element.5.res_in), custom_call_target="tpu_custom_call" | custom-call | tf_op jit(solution)/shard_map/finish/pallas_call | solution.py:533
